TPU v7x, 32 devices: a whole 2x2x4 slice. The times are simulated.
32 devices in a mesh: lat: 8 (over z, y), ch: 4 (over x, core).
Axes of the slice: x: 2, y: 2, z: 4, core: 2. Of those that a mesh axis runs over, the one named last changes fastest.
Arguments:
- field: bfloat16 [728, 256, 1440], P('lat', 'ch'), may hold values from -6 to 6
- legendre: bfloat16 [384, 721, 728], P(('lat', 'ch')), may hold values from -0.21875 to 0.21875
- pair_order: int32 [384], replicated, may hold values from 0 to 383, each once
Outputs:
- coeffs: float32 [384, 721, 2, 256], P(('lat', 'ch'))
Inputs may be any that keep to these rules, and one draw needn't show every extreme that they name: `pair_order`: each of 0 to 383 appears once; a value p below 360 gives its bin the orders p and 719 - p, and a bin with a larger value is empty.
All inputs are finite; a program needn't handle non-finite values.
Results may differ from a plain program's by a relative error of at most 0.0037.
Values may be sent and summed in bfloat16 or wider, within the bound.
A program may use at most 256 MiB of HBM per device.

v0:
```python
import math
import jax
import jax.numpy as jnp
from jax import lax
from jax.sharding import PartitionSpec as P

NLAT = 721


def dft_table(points, modes, lon_count):
    turns = points[:, None] * modes[None, :] % lon_count
    angle = turns.astype(jnp.float32) * (2.0 * math.pi / lon_count)
    return jnp.stack([jnp.cos(angle), -jnp.sin(angle)], axis=-1).astype(jnp.bfloat16)


def project(basis_piece, data_rows, boundary, keep_mask):
    products = jnp.einsum(
        "brl,lbn->brn", basis_piece, data_rows, preferred_element_type=jnp.float32
    )
    bin_count, row_count, width_all = products.shape
    products = products.reshape(bin_count, row_count, 2, 2, width_all // 4)
    degree = jnp.arange(row_count, dtype=jnp.int32)
    upper_part = degree[None, :, None, None] < boundary[:, None, None, None]
    chosen = jnp.where(upper_part, products[:, :, 0], products[:, :, 1])
    return chosen * keep_mask[:, None, None, None].astype(jnp.float32)


def per_device(field, legendre, pair_order):
    lat_rows, chan_dev, lon_count = field.shape
    slot_count = pair_order.shape[0]
    lat_count = lax.axis_size("lat")
    group_size = slot_count // lat_count
    max_order = legendre.shape[1] - 1
    keep_all = pair_order < max_order // 2
    first_order = jnp.where(keep_all, pair_order, 0)
    orders = jnp.stack([first_order, max_order - 1 - first_order], axis=1)
    bound_all = max_order - first_order
    rows_global = lax.axis_index("lat") * lat_rows + jnp.arange(lat_rows, dtype=jnp.int32)
    masked = jnp.where((rows_global < NLAT)[:, None, None], field, jnp.zeros_like(field))
    norm_scale = 2.0 * math.pi / lon_count
    points = jnp.arange(lon_count, dtype=jnp.int32)
    dft_basis = dft_table(points, orders.reshape(-1), lon_count).reshape(lon_count, 4 * slot_count)
    fourier = jnp.einsum("ack,kn->anc", masked, dft_basis, preferred_element_type=jnp.float32)
    fourier = (fourier * norm_scale).astype(jnp.bfloat16).reshape(lat_rows, slot_count, 4, chan_dev)
    received = lax.all_to_all(
        fourier.reshape(lat_rows, slot_count, 4 * chan_dev),
        "lat",
        split_axis=1,
        concat_axis=0,
        tiled=True,
    )
    group_start = lax.axis_index("lat") * group_size
    bound_group = lax.dynamic_slice_in_dim(bound_all, group_start, group_size)
    keep_group = lax.dynamic_slice_in_dim(keep_all, group_start, group_size)
    part_sums = project(
        lax.all_gather(legendre, "ch", axis=0, tiled=True), received, bound_group, keep_group
    )
    return lax.all_to_all(part_sums, "ch", split_axis=0, concat_axis=3, tiled=True)


def solution(mesh):
    in_specs = (P("lat", "ch", None), P(("lat", "ch"), None, None), P())
    out_specs = P(("lat", "ch"), None, None, None)
    return jax.shard_map(
        per_device, mesh=mesh, in_specs=in_specs, out_specs=out_specs, check_vma=False
    )
```

profile of v0, /device:TPU:0, one launch (start us, length us, event | category | flops | bytes accessed | tf_op | source)
XLA Modules:
  0.0 950.9 jit_solution(16822089257262218695)
XLA Ops:
  6.5 0.7 all-gather.2.cloned.1.call-update
  7.3 0.7 broadcast_subtract_fusion.1
  8.0 0.1 copy.30
  8.1 0.1 mul.66
  8.3 19.0 %cosine_convert_fusion = (bf16[1440,768,1]{1,0,2:T(8,128)(2,1)S(1)}, bf16[1440,768,1]{1,0,2:T(8,128)(2,1)S(1)}) fusion(s32[768]{0:T(1024)S(1)} %mul.66), kind=kLoop, calls=%fused_computation.18 | loop fusion | flops 13271040 | bytes 4426752 | tf_op jit(solution)/shard_map/convert
  27.3 3.2 pad_maximum_fusion
  30.6 13.2 %copy.31 = bf16[1440,768,2]{0,2,1:T(2,128)(2,1)} copy(bf16[1440,768,2]{1,0,2:T(8,128)(2,1)} %pad_maximum_fusion) | data formatting | bytes 8847360 | tf_op jit(solution)/shard_map/stack | solution.py:13
  43.8 10.9 %convert_element_type.30 = bf16[1440,1536]{0,1:T(8,128)(2,1)} reshape(bf16[1440,768,2]{0,2,1:T(2,128)(2,1)} %copy.31) | data formatting | bytes 8847360 | tf_op jit(solution)/shard_map/convert_element_type | solution.py:13
  54.7 16.6 %broadcast_select_fusion = bf16[91,64,1440]{2,1,0:T(8,128)(2,1)} fusion(bf16[91,64,1440]{2,1,0:T(8,128)(2,1)} %param.3, pred[91]{0:T(512)(128)(4,1)S(1)} %add_compare_fusion), kind=kLoop, calls=%fused_computation.10 | loop fusion | flops 8386560 | bytes 33546332 | tf_op jit(solution)/shard_map/jit(_where)/select_n | solution.py:39
  71.3 49.8 %fusion = bf16[91,1536,64]{1,0,2:T(8,128)(2,1)} fusion(bf16[91,64,1440]{2,1,0:T(8,128)(2,1)} %broadcast_select_fusion, bf16[1440,1536]{0,1:T(8,128)(2,1)S(1)} %copy-done), kind=kOutput, calls=%fused_computation.1 | convolution fusion | flops 25781403648 | bytes 39088128 | tf_op jit(solution)/shard_map/ack,kn->anc/dot_general | solution.py:43
  121.2 31.3 %copy.34 = bf16[91,1536,64]{0,2,1:T(8,128)(2,1)} copy(bf16[91,1536,64]{1,0,2:T(8,128)(2,1)} %fusion) | data formatting | bytes 35782656 | tf_op jit(solution)/shard_map/convert_element_type | solution.py:44
  152.5 28.4 %copy.35 = bf16[91,384,256]{2,0,1:T(8,128)(2,1)} copy(bf16[91,384,256]{0,2,1:T(8,128)(2,1)} %bitcast.33) | data formatting | bytes 35782656 | tf_op jit(solution)/shard_map/reshape;reshape | solution.py:46
  180.9 7.3 all-to-all-start
  188.1 0.1 dynamic_slice.6
  188.2 0.1 dynamic-slice_convert_fusion
  188.3 0.1 iota_compare_fusion
  188.4 408.6 %all-to-all-done = bf16[91,384,256]{2,0,1:T(8,128)(2,1)} async-done(((bf16[91,384,256]{2,0,1:T(8,128)(2,1)}), bf16[91,384,256]{2,0,1:T(8,128)(2,1)}, u32[]{:S(2)}, u32[]{:S(2)}) %all-to-all-start) | async-done | bytes 17891360 | tf_op jit(solution)/shard_map/all_to_all | solution.py:45
  596.9 19.0 %copy.37 = bf16[8,91,48,256]{3,2,1,0:T(8,128)(2,1)} copy(bf16[8,91,48,256]{3,1,2,0:T(8,128)(2,1)} %bitcast.5) | data formatting | bytes 35782656 | tf_op jit(solution)/shard_map/all_to_all | solution.py:45
  615.9 36.0 %fusion.9 = f32[48,721,256]{2,1,0:T(8,128)} fusion(bf16[48,721,728]{2,1,0:T(8,128)(2,1)} %all-gather.2.cloned.1.call-done, bf16[728,48,256]{2,1,0:T(8,128)(2,1)} %bitcast.36), kind=kOutput, calls=%fused_computation.11 | convolution fusion | flops 12899647488 | bytes 103719168 | tf_op jit(solution)/shard_map/brl,lbn->brn/dot_general | solution.py:17
  651.9 36.0 %copy.39 = f32[48,721,256]{1,2,0:T(8,128)} copy(f32[48,721,256]{2,1,0:T(8,128)} %fusion.9) | data formatting | bytes 70877184 | tf_op jit(solution)/shard_map/brl,lbn->brn/dot_general | solution.py:17
  687.9 12.8 %fusion.2 = f32[48,721,2,64]{1,3,2,0:T(8,128)S(1)} fusion(f32[48,721,2,2,64]{1,4,3,2,0:T(8,128)} %bitcast.32, f32[48]{0:T(128)S(1)} %dynamic-slice_convert_fusion, pred[48,721]{1,0:T(8,128)(4,1)S(1)} %iota_compare_fusion), kind=kLoop, calls=%fused_computation.4 | loop fusion | flops 8859648 | bytes 53192688 | tf_op jit(solution)/shard_map/mul | solution.py:25
  700.8 208.6 %all_to_all.36 = f32[48,721,2,64]{1,3,2,0:T(8,128)S(1)} all-to-all(f32[48,721,2,64]{1,3,2,0:T(8,128)S(1)} %fusion.2), channel_id=1, replica_groups=mesh['lat'=8,'ch'=4] {'ch'}, dimensions={0} | all-to-all | bytes 35438592 | tf_op jit(solution)/shard_map/all_to_all | solution.py:58
  909.4 6.9 copy.41
  916.4 27.7 %copy.42 = f32[12,721,2,256]{3,2,1,0:T(2,128)} copy(f32[12,721,2,256]{1,3,2,0:T(8,128)} %bitcast.35) | data formatting | bytes 35438592 | tf_op jit(solution)/shard_map/all_to_all | solution.py:58
  (11 shorter events, 0.0 us)
Async XLA Ops:
  6.5 609.4 %all-gather.2.cloned.1.call-start = ((), (), s32[]{:S(2)}) async-start(), calls=%async_computation.2 | async-start | bytes 67092480 | tf_op jit(solution)/shard_map/all_gather | solution.py:56
  54.7 16.6 %copy-start = (bf16[1440,1536]{0,1:T(8,128)(2,1)S(1)}, bf16[1440,1536]{0,1:T(8,128)(2,1)}, u32[]{:S(2)}) copy-start(bf16[1440,1536]{0,1:T(8,128)(2,1)} %convert_element_type.30) | copy-start | bytes 13271044
  180.9 7.3 copy-start.1
  180.9 416.1 %all-to-all-start = ((bf16[91,384,256]{2,0,1:T(8,128)(2,1)}), bf16[91,384,256]{2,0,1:T(8,128)(2,1)}, u32[]{:S(2)}, u32[]{:S(2)}) async-start(bf16[91,384,256]{2,0,1:T(8,128)(2,1)} %copy.35), calls=%async_computation | async-start | bytes 37748736 | tf_op jit(solution)/shard_map/all_to_all | solution.py:45
Sparse Core Ops, SparseCore 0:
  8.9 320.7 all-gather.1
where the time goes:
time: 955 us; the launch traced here: 951 us
  waiting for transfers between devices  409 us (43%)
  blocking collectives  209 us (22%)
  local copies, waits for them, and re-layouts  174 us (18%)
  matrix products  85.8 us (9%)
  other arithmetic  52.6 us (6%)
  between operations  13.4 us (1%)
    all_to_all x1, waiting for transfers between devices, per_device(): lax.all_to_all(fourier.reshape(lat_rows, slot_count, 4 * chan_dev), 'lat'...  409 us
    all_to_all x1, blocking collectives, per_device(): lax.all_to_all(part_sums, 'ch', split_axis=0, concat_axis=3, tiled=True)  209 us
    dot_general x1, matrix products, per_device(): jnp.einsum('ack,kn->anc', masked, dft_basis, preferred_element_type=jnp.f...  49.8 us
    dot_general x1, local copies, waits for them, and re-layouts, project(): jnp.einsum('brl,lbn->brn', basis_piece, data_rows, preferred_element_type...  36 us
    dot_general x1, matrix products, project(): jnp.einsum('brl,lbn->brn', basis_piece, data_rows, preferred_element_type...  36 us
    all_to_all x2, local copies, waits for them, and re-layouts, per_device(): lax.all_to_all(part_sums, 'ch', split_axis=0, concat_axis=3, tiled=True)  34.7 us
    convert_element_type x1, local copies, waits for them, and re-layouts, per_device(): (fourier * norm_scale).astype(jnp.bfloat16)  31.3 us
    another operation x1, local copies, waits for them, and re-layouts, per_device(): fourier.reshape(lat_rows, slot_count, 4 * chan_dev)  28.4 us
  transfers between devices with their start and end apart: 2, of which 1 were waited for; matrix products, arithmetic and copies ran while one was open for 20% of the time, Pallas kernels for 0%

commit v1 on v0

--- a/solution.py
+++ b/solution.py
@@ -42,12 +42,20 @@
     dft_basis = dft_table(points, orders.reshape(-1), lon_count).reshape(lon_count, 4 * slot_count)
     fourier = jnp.einsum("ack,kn->anc", masked, dft_basis, preferred_element_type=jnp.float32)
     fourier = (fourier * norm_scale).astype(jnp.bfloat16).reshape(lat_rows, slot_count, 4, chan_dev)
-    received = lax.all_to_all(
-        fourier.reshape(lat_rows, slot_count, 4 * chan_dev),
-        "lat",
-        split_axis=1,
-        concat_axis=0,
-        tiled=True,
+    received = jnp.concatenate(
+        lax.all_to_all(
+            jnp.stack(
+                jnp.split(
+                    fourier.reshape(lat_rows, slot_count, 4 * chan_dev),
+                    lax.axis_size("lat"),
+                    axis=1,
+                )
+            ),
+            "lat",
+            0,
+            0,
+        ),
+        axis=0,
     )
     group_start = lax.axis_index("lat") * group_size
     bound_group = lax.dynamic_slice_in_dim(bound_all, group_start, group_size)

time: 955 us -> 941 us (0.985)
  waiting for transfers between devices: 409 us -> 388 us
    unnamed x4 -> x13, local copies, waits for them, and re-layouts: 0.01 us -> 23.6 us
    all_to_all x1, waiting for transfers between devices: 409 us -> 387 us  [per_device(): lax.all_to_all(jnp.stack(jnp.split(fourier.reshape(lat_rows, slot_count,...]
    all_to_all x1 -> x0, local copies, waits for them, and re-layouts: 19 us -> none  [per_device(): lax.all_to_all(fourier.reshape(lat_rows, slot_count, 4 * chan_dev), 'lat'...]
    another operation x1 -> x2, local copies, waits for them, and re-layouts: 28.4 us -> 31.9 us  [per_device(): jnp.stack(jnp.split(fourier.reshape(lat_rows, slot_count, 4 * chan_dev),...]
  transfers between devices with their start and end apart: 2 -> 2, of which waited for: 1 -> 1; matrix products, arithmetic and copies ran while one was open for 20% -> 21% of each run, Pallas kernels for 0% -> 0%
where the time goes in v1:
time: 941 us; the launch traced here: 937 us
  waiting for transfers between devices  388 us (41%)
  blocking collectives  209 us (22%)
  local copies, waits for them, and re-layouts  182 us (19%)
  matrix products  85.8 us (9%)
  other arithmetic  52.6 us (6%)
  between operations  13.4 us (1%)
    all_to_all x1, waiting for transfers between devices, per_device(): lax.all_to_all(jnp.stack(jnp.split(fourier.reshape(lat_rows, slot_count,...  387 us
    all_to_all x1, blocking collectives, per_device(): lax.all_to_all(part_sums, 'ch', split_axis=0, concat_axis=3, tiled=True)  209 us
    dot_general x1, matrix products, per_device(): jnp.einsum('ack,kn->anc', masked, dft_basis, preferred_element_type=jnp.f...  49.8 us
    dot_general x1, local copies, waits for them, and re-layouts, project(): jnp.einsum('brl,lbn->brn', basis_piece, data_rows, preferred_element_type...  36 us
    dot_general x1, matrix products, project(): jnp.einsum('brl,lbn->brn', basis_piece, data_rows, preferred_element_type...  36 us
    all_to_all x2, local copies, waits for them, and re-layouts, per_device(): lax.all_to_all(part_sums, 'ch', split_axis=0, concat_axis=3, tiled=True)  34.7 us
    another operation x2, local copies, waits for them, and re-layouts, per_device(): jnp.stack(jnp.split(fourier.reshape(lat_rows, slot_count, 4 * chan_dev),...  31.9 us
    convert_element_type x1, local copies, waits for them, and re-layouts, per_device(): (fourier * norm_scale).astype(jnp.bfloat16)  31.3 us
  transfers between devices with their start and end apart: 2, of which 1 were waited for; matrix products, arithmetic and copies ran while one was open for 21% of the time, Pallas kernels for 0%

profile of v1, /device:TPU:0, one launch (start us, length us, event | category | flops | bytes accessed | tf_op | source)
XLA Modules:
  0.0 937.2 jit_solution(6972195727442938743)
XLA Ops:
  8.3 19.0 %cosine_convert_fusion = (bf16[1440,768,1]{1,0,2:T(8,128)(2,1)S(1)}, bf16[1440,768,1]{1,0,2:T(8,128)(2,1)S(1)}) fusion(s32[768]{0:T(1024)S(1)} %mul.66), kind=kLoop, calls=%fused_computation.18 | loop fusion | flops 13271040 | bytes 4426752 | tf_op jit(solution)/shard_map/convert
  27.3 3.2 pad_maximum_fusion
  30.6 13.2 %copy.35 = bf16[1440,768,2]{0,2,1:T(2,128)(2,1)} copy(bf16[1440,768,2]{1,0,2:T(8,128)(2,1)} %pad_maximum_fusion) | data formatting | bytes 8847360 | tf_op jit(solution)/shard_map/stack | solution.py:13
  43.8 10.9 %convert_element_type.30 = bf16[1440,1536]{0,1:T(8,128)(2,1)} reshape(bf16[1440,768,2]{0,2,1:T(2,128)(2,1)} %copy.35) | data formatting | bytes 8847360 | tf_op jit(solution)/shard_map/convert_element_type | solution.py:13
  54.7 16.6 %broadcast_select_fusion = bf16[91,64,1440]{2,1,0:T(8,128)(2,1)} fusion(bf16[91,64,1440]{2,1,0:T(8,128)(2,1)} %param.3, pred[91]{0:T(512)(128)(4,1)S(1)} %add_compare_fusion), kind=kLoop, calls=%fused_computation.10 | loop fusion | flops 8386560 | bytes 33546332 | tf_op jit(solution)/shard_map/jit(_where)/select_n | solution.py:39
  71.4 49.8 %fusion = bf16[91,1536,64]{1,0,2:T(8,128)(2,1)} fusion(bf16[91,64,1440]{2,1,0:T(8,128)(2,1)} %broadcast_select_fusion, bf16[1440,1536]{0,1:T(8,128)(2,1)S(1)} %copy-done.1), kind=kOutput, calls=%fused_computation.1 | convolution fusion | flops 25781403648 | bytes 39088128 | tf_op jit(solution)/shard_map/ack,kn->anc/dot_general | solution.py:43
  121.2 31.3 %copy.38 = bf16[91,1536,64]{0,2,1:T(8,128)(2,1)} copy(bf16[91,1536,64]{1,0,2:T(8,128)(2,1)} %fusion) | data formatting | bytes 35782656 | tf_op jit(solution)/shard_map/convert_element_type | solution.py:44
  152.5 4.2 fusion.25
  156.7 4.6 fusion.24
  161.3 4.7 fusion.23
  166.0 3.9 fusion.22
  169.9 2.0 fusion.21
  171.9 2.2 fusion.20
  174.1 2.0 fusion.19
  176.1 2.0 fusion.18
  178.1 29.9 %copy.39 = bf16[8,91,48,256]{3,2,1,0:T(8,128)(2,1)} copy(bf16[8,91,48,256]{1,3,2,0:T(8,128)(2,1)} %fusion.18) | data formatting | bytes 35782656 | tf_op jit(solution)/shard_map/stack | solution.py:47
  208.0 7.1 all-to-all-start
  215.4 386.8 %all-to-all-done = bf16[8,91,48,256]{3,2,1,0:T(8,128)(2,1)} async-done(((bf16[8,91,48,256]{3,2,1,0:T(8,128)(2,1)}), bf16[8,91,48,256]{3,2,1,0:T(8,128)(2,1)}, u32[]{:S(2)}, u32[]{:S(2)}) %all-to-all-start) | async-done | bytes 17891360 | tf_op jit(solution)/shard_map/all_to_all | solution.py:46
  602.2 36.0 %fusion.9 = f32[48,721,256]{2,1,0:T(8,128)} fusion(bf16[48,721,728]{2,1,0:T(8,128)(2,1)} %all-gather.2.cloned.1.call-done, bf16[728,48,256]{2,1,0:T(8,128)(2,1)} %bitcast.11), kind=kOutput, calls=%fused_computation.11 | convolution fusion | flops 12899647488 | bytes 103719168 | tf_op jit(solution)/shard_map/brl,lbn->brn/dot_general | solution.py:17
  638.2 36.0 %copy.41 = f32[48,721,256]{1,2,0:T(8,128)} copy(f32[48,721,256]{2,1,0:T(8,128)} %fusion.9) | data formatting | bytes 70877184 | tf_op jit(solution)/shard_map/brl,lbn->brn/dot_general | solution.py:17
  674.3 12.8 %fusion.2 = f32[48,721,2,64]{1,3,2,0:T(8,128)S(1)} fusion(f32[48,721,2,2,64]{1,4,3,2,0:T(8,128)} %bitcast.61, f32[48]{0:T(128)S(1)} %dynamic-slice_convert_fusion, pred[48,721]{1,0:T(8,128)(4,1)S(1)} %iota_compare_fusion), kind=kLoop, calls=%fused_computation.4 | loop fusion | flops 8859648 | bytes 53192688 | tf_op jit(solution)/shard_map/mul | solution.py:25
  687.1 208.6 %all_to_all.23 = f32[48,721,2,64]{1,3,2,0:T(8,128)S(1)} all-to-all(f32[48,721,2,64]{1,3,2,0:T(8,128)S(1)} %fusion.2), channel_id=1, replica_groups=mesh['lat'=8,'ch'=4] {'ch'}, dimensions={0} | all-to-all | bytes 35438592 | tf_op jit(solution)/shard_map/all_to_all | solution.py:66
  895.7 6.9 copy.43
  902.7 27.7 %copy.44 = f32[12,721,2,256]{3,2,1,0:T(2,128)} copy(f32[12,721,2,256]{1,3,2,0:T(8,128)} %bitcast.71) | data formatting | bytes 35438592 | tf_op jit(solution)/shard_map/all_to_all | solution.py:66
  (20 shorter events, 2.0 us)
Async XLA Ops:
  6.5 595.7 %all-gather.2.cloned.1.call-start = ((), (), s32[]{:S(2)}) async-start(), calls=%async_computation.2 | async-start | bytes 67092480 | tf_op jit(solution)/shard_map/all_gather | solution.py:64
  54.7 16.6 %copy-start.1 = (bf16[1440,1536]{0,1:T(8,128)(2,1)S(1)}, bf16[1440,1536]{0,1:T(8,128)(2,1)}, u32[]{:S(2)}) copy-start(bf16[1440,1536]{0,1:T(8,128)(2,1)} %convert_element_type.30) | copy-start | bytes 13271044
  152.5 17.4 %copy-start = (bf16[91,1536,64]{0,2,1:T(8,128)(2,1)S(1)}, bf16[91,1536,64]{0,2,1:T(8,128)(2,1)}, u32[]{:S(2)}) copy-start(bf16[91,1536,64]{0,2,1:T(8,128)(2,1)} %copy.38) | copy-start | bytes 53673988
  208.0 7.2 copy-start.2
  208.0 394.2 %all-to-all-start = ((bf16[8,91,48,256]{3,2,1,0:T(8,128)(2,1)}), bf16[8,91,48,256]{3,2,1,0:T(8,128)(2,1)}, u32[]{:S(2)}, u32[]{:S(2)}) async-start(bf16[8,91,48,256]{3,2,1,0:T(8,128)(2,1)} %copy.39), calls=%async_computation | async-start | bytes 35782656 | tf_op jit(solution)/shard_map/all_to_all | solution.py:46
Sparse Core Ops, SparseCore 0:
  8.9 320.7 all-gather.1
